TPU v7x, 32 devices: a whole 2x2x4 slice. The times are simulated.
32 devices in a mesh: tile: 8 (over y, x, core), lev: 4 (over z).
Axes of the slice: x: 2, y: 2, z: 4, core: 2. Of those that a mesh axis runs over, the one named last changes fastest.
Arguments:
- members_pert: bfloat16 [64, 16, 32768], P('lev', None, 'tile'), may hold values from -4 to 4
- coarse_pert: bfloat16 [64, 8, 2048], P('lev', None, 'tile'), may hold values from -6 to 6
- member_ctrl: bfloat16 [64, 16, 2048], P('lev', None, 'tile'), may hold values from -6 to 6
- coarse_ctrl: bfloat16 [64, 8, 2048], P('lev', None, 'tile'), may hold values from -6 to 6
- vert_loc: float32 [64, 64], replicated, may hold values from -1.5 to 1.5, as said below
- stencil: int32 [4, 32768], P(None, 'tile'), may hold values from 0 to 383, as said below
- interp_w: bfloat16 [4, 32768], P(None, 'tile'), may hold values from 0 to 1, as said below
Outputs:
- member_out: float32 [64, 16, 2048], P('lev', None, 'tile')
- coarse_out: float32 [64, 8, 2048], P('lev', None, 'tile')
Inputs may be any that keep to these rules, and one draw needn't show every extreme that they name: vert_loc[i, j] is zero where |i - j| > 4, and nonzero where |i - j| = 4. stencil indexes a window of 384 coarse cells of the fine cell's tile index: the last 64 coarse cells of the tile index before it (the first one's predecessor is the last), its own 256 cells, then the first 64 cells of the tile index after it; the four corners of a fine cell are distinct. `interp_w`: the four weights of a fine cell are nonnegative and sum to one up to rounding.
All inputs are finite; a program needn't handle non-finite values.
Results may differ from a plain program's by a relative error of at most 0.013.
Values may be sent and summed in bfloat16 or wider, within the bound.
A program may use at most 64 MiB of HBM per device.

v0:
```python
import jax
import jax.numpy as jnp
from jax import lax
from jax.sharding import PartitionSpec as P

HB = 4
CW = 64


def extended(value, sides, width, wrap):
    for axis, dim in sides:
        size, length = (lax.axis_size(axis), value.shape[dim])
        up = [(i, (i + 1) % size) for i in range(size if wrap else size - 1)]
        down = [(j, i) for i, j in up]
        last = lax.slice_in_dim(value, length - width, length, axis=dim)
        leading = lax.slice_in_dim(value, 0, width, axis=dim)
        before = lax.ppermute(last, axis, up)
        after = lax.ppermute(leading, axis, down)
        value = jnp.concatenate([before, value, after], axis=dim)
    return value


def shifted(value, axis, by):
    size = lax.axis_size(axis)
    return lax.ppermute(value, axis, [(i, (i + by) % size) for i in range(size)])


def from_behind(value, axis, by):
    size = lax.axis_size(axis)
    pairs = [(i, i + by) for i in range(size) if 0 <= i + by < size]
    return lax.ppermute(value, axis, pairs)


def shards(members_pert, coarse_pert, member_ctrl, coarse_ctrl, vert_loc, stencil, interp_w):
    highest = lax.Precision.HIGHEST
    level_rows = member_ctrl.shape[0]
    members = member_ctrl.shape[1]
    coarse_cells = member_ctrl.shape[2]
    fine_cells = members_pert.shape[2]
    kinds = members + 1
    stacked = jnp.concatenate([member_ctrl, coarse_ctrl], axis=1)
    widened = extended(stacked, (("lev", 0),), HB, False)
    first_level = lax.axis_index("lev") * level_rows
    padded = jnp.pad(vert_loc, ((0, 0), (HB, HB)))
    band_rows = lax.dynamic_slice(
        padded, (first_level, first_level), (level_rows, level_rows + 2 * HB)
    )
    localized = jnp.einsum("ij,jkc->ikc", band_rows, widened.astype(jnp.float32), precision=highest)
    loc_members = localized[:, :members].astype(jnp.bfloat16)
    loc_coarse = localized[:, members:].astype(jnp.bfloat16)
    combined = jnp.sum(
        coarse_pert.astype(jnp.float32) * loc_coarse.astype(jnp.float32), axis=1
    ).astype(jnp.bfloat16)
    fields = jnp.concatenate([loc_members, combined[:, None, :]], axis=1)
    window = extended(fields, (("tile", 2),), CW, True)
    window_span = window.shape[2]
    cell_rows = lax.broadcasted_iota(jnp.int32, (window_span, fine_cells), 0)
    nothing = jnp.zeros((), jnp.bfloat16)
    interp_matrix = jnp.zeros((window_span, fine_cells), jnp.bfloat16)
    for corner in range(4):
        interp_matrix = interp_matrix + jnp.where(
            cell_rows == stencil[corner][None, :], interp_w[corner][None, :], nothing
        )
    flattened = window.reshape(level_rows * kinds, window_span)
    interp = jnp.dot(flattened, interp_matrix, preferred_element_type=jnp.float32).reshape(
        level_rows, kinds, fine_cells
    )
    pert_float = members_pert.astype(jnp.float32)
    increment = jnp.sum(pert_float * interp[:, :members], axis=1) + interp[:, members]
    adjoint = jnp.concatenate(
        [pert_float * increment[:, None, :], increment[:, None, :]], axis=1
    ).astype(jnp.bfloat16)
    coarse_adjoint = lax.dot_general(
        adjoint.reshape(level_rows * kinds, fine_cells),
        interp_matrix,
        (((1,), (1,)), ((), ())),
        preferred_element_type=jnp.float32,
    )
    coarse_adjoint = coarse_adjoint.reshape(level_rows, kinds, window_span)
    own_cells = coarse_adjoint[:, :, CW : CW + coarse_cells]
    from_next = shifted(coarse_adjoint[:, :, :CW].astype(jnp.bfloat16), "tile", -1).astype(
        jnp.float32
    )
    from_prev = shifted(
        coarse_adjoint[:, :, CW + coarse_cells :].astype(jnp.bfloat16), "tile", 1
    ).astype(jnp.float32)
    gathered = (
        own_cells
        + jnp.pad(from_next, ((0, 0), (0, 0), (coarse_cells - CW, 0)))
        + jnp.pad(from_prev, ((0, 0), (0, 0), (0, coarse_cells - CW)))
    )
    adjoint_ctrl = jnp.concatenate(
        [
            gathered[:, :members],
            coarse_pert.astype(jnp.float32) * gathered[:, members : members + 1],
        ],
        axis=1,
    )
    spread = jnp.einsum("ij,ikc->jkc", band_rows, adjoint_ctrl, precision=highest)
    from_above = from_behind(spread[:HB].astype(jnp.bfloat16), "lev", -1).astype(jnp.float32)
    from_below = from_behind(spread[level_rows + HB :].astype(jnp.bfloat16), "lev", 1).astype(
        jnp.float32
    )
    result = spread[HB : HB + level_rows]
    result = result + jnp.pad(from_below, ((0, level_rows - HB), (0, 0), (0, 0)))
    result = result + jnp.pad(from_above, ((level_rows - HB, 0), (0, 0), (0, 0)))
    return (result[:, :members], result[:, members:])


def solution(mesh):
    in_specs = (
        P("lev", None, "tile"),
        P("lev", None, "tile"),
        P("lev", None, "tile"),
        P("lev", None, "tile"),
        P(),
        P(None, "tile"),
        P(None, "tile"),
    )
    out_specs = (P("lev", None, "tile"), P("lev", None, "tile"))
    return jax.shard_map(shards, mesh=mesh, in_specs=in_specs, out_specs=out_specs, check_vma=False)
```

profile of v0, /device:TPU:0, one launch (start us, length us, event | category | flops | bytes accessed | tf_op | source)
XLA Modules:
  0.0 50.5 jit_solution(11638122476476656988)
XLA Ops:
  0.6 0.9 %copy_dynamic-update-slice_fusion = bf16[16,24,256]{2,0,1:T(8,128)(2,1)S(1)} fusion(bf16[16,16,256]{2,1,0:T(8,128)(2,1)} %param.9), kind=kLoop, calls=%fused_computation.43 | loop fusion | bytes 262144
  1.6 0.9 %copy_dynamic-update-slice_fusion.1 = bf16[16,24,256]{2,0,1:T(8,128)(2,1)S(1)} fusion(bf16[16,24,256]{2,0,1:T(8,128)(2,1)S(1)} %copy_dynamic-update-slice_fusion, bf16[16,8,256]{2,1,0:T(8,128)(2,1)} %param.10), kind=kLoop, calls=%fused_computation.46 | loop fusion | bytes 131072 | tf_op jit(solution)/shard_map/concatenate | solution.py:41
  2.5 5.0 %collective-permute-start = (bf16[4,24,256]{2,0,1:T(4,128)(2,1)S(1)}, bf16[4,24,256]{2,0,1:T(4,128)(2,1)S(1)}, u32[]{:S(2)}, u32[]{:S(2)}) collective-permute-start(bf16[4,24,256]{2,0,1:T(4,128)(2,1)S(1)} %get-tuple-element.14), channel_id=1, source_target_pairs={{0,1},{1,2},{2,3},{4,5},{5,6},{6,7},{8,9},{9,10},{10,11},{12,13},{... | collective-permute-start | bytes 147464 | tf_op jit(solution)/shard_map/ppermute | solution.py:17
  7.5 1.3 %collective-permute-start.1 = (bf16[4,24,256]{2,0,1:T(4,128)(2,1)S(1)}, bf16[4,24,256]{2,0,1:T(4,128)(2,1)S(1)}, u32[]{:S(2)}, u32[]{:S(2)}) collective-permute-start(bf16[4,24,256]{2,0,1:T(4,128)(2,1)S(1)} %get-tuple-element.15), channel_id=1, source_target_pairs={{1,0},{2,1},{3,2},{5,4},{6,5},{7,6},{9,8},{10,9},{11,10},{13,12},{... | collective-permute-start | bytes 147464 | tf_op jit(solution)/shard_map/ppermute | solution.py:18
  8.8 1.1 %fusion.42 = (s32[1,4096]{1,0:T(1,128)S(1)}, s32[1,4096]{1,0:T(1,128)S(1)}, s32[1,4096]{1,0:T(1,128)S(1)}, s32[1,4096]{1,0:T(1,128)S(1)}) fusion(s32[4,4096]{1,0:T(4,128)} %param.12), kind=kLoop, calls=%fused_computation.65 | loop fusion | bytes 131072 | tf_op jit(solution)/shard_map/slice | solution.py:62
  9.8 0.0 collective-permute-done
  9.8 3.6 %collective-permute-done.1 = bf16[4,24,256]{2,0,1:T(4,128)(2,1)S(1)} collective-permute-done((bf16[4,24,256]{2,0,1:T(4,128)(2,1)S(1)}, bf16[4,24,256]{2,0,1:T(4,128)(2,1)S(1)}, u32[]{:S(2)}, u32[]{:S(2)}) %collective-permute-start.1) | collective-permute-done | bytes 49184 | tf_op jit(solution)/shard_map/ppermute | solution.py:18
  13.4 1.1 %convolution_convert_fusion = bf16[16,24,256]{2,0,1:T(8,128)(2,1)S(1)} fusion(bf16[4,24,256]{2,0,1:T(4,128)(2,1)S(1)} %collective-permute-done.1, bf16[16,24,256]{2,0,1:T(8,128)(2,1)S(1)} %copy_dynamic-update-slice_fusion.1, bf16[4,24,256]{2,0,1:T(4,128)(2,1)S(1)} %collective-permute-done, s32[]{:T(128)S(6)} %select_n.19, s32[]{:T(128)S(6)} %select_n.20, ...), kind=kOutput, calls=%fused_computation.21 | convolution fusion | flops 29294592 | bytes 507912 | tf_op jit(solution)/shard_map/ij,jkc->ikc/dot_general | solution.py:48
  14.6 0.9 %fusion.27 = bf16[16,256]{1,0:T(8,128)(2,1)S(1)} fusion(bf16[16,24,256]{2,0,1:T(8,128)(2,1)S(1)} %convolution_convert_fusion, bf16[16,8,256]{2,1,0:T(8,128)(2,1)} %param.8), kind=kLoop, calls=%fused_computation.42 | loop fusion | flops 126976 | bytes 139264 | tf_op jit(solution)/shard_map/reduce_sum | solution.py:51
  15.4 0.1 fusion.28
  15.5 0.1 collective-permute-start.2
  15.6 2.6 %collective-permute-start.3 = (bf16[16,17,64]{2,0,1:T(8,128)(2,1)S(1)}, bf16[16,17,64]{2,0,1:T(8,128)(2,1)S(1)}, u32[]{:S(2)}, u32[]{:S(2)}) collective-permute-start(bf16[16,17,64]{2,0,1:T(8,128)(2,1)S(1)} %get-tuple-element.17), channel_id=1, source_target_pairs={{4,0},{8,4},{12,8},{16,12},{20,16},{24,20},{28,24},{0,28},{5,1},{9... | collective-permute-start | bytes 104456 | tf_op jit(solution)/shard_map/ppermute | solution.py:18
  18.2 1.1 %slice_reduce_fusion.3 = (bf16[4096]{0:T(1024)(128)(2,1)S(1)}, bf16[4096]{0:T(1024)(128)(2,1)S(1)}, bf16[4096]{0:T(1024)(128)(2,1)S(1)}, bf16[4096]{0:T(1024)(128)(2,1)S(1)}) fusion(bf16[4,4096]{1,0:T(4,128)(2,1)} %param.13), kind=kLoop, calls=%fused_computation.52 | loop fusion | bytes 65536 | tf_op jit(solution)/shard_map/slice | solution.py:62
  19.3 0.9 %collective-permute-done.2 = bf16[16,17,64]{2,0,1:T(8,128)(2,1)S(1)} collective-permute-done((bf16[16,17,64]{2,0,1:T(8,128)(2,1)S(1)}, bf16[16,17,64]{2,0,1:T(8,128)(2,1)S(1)}, u32[]{:S(2)}, u32[]{:S(2)}) %collective-permute-start.2) | collective-permute-done | bytes 34848 | tf_op jit(solution)/shard_map/ppermute | solution.py:17
  20.2 0.0 collective-permute-done.3
  20.2 0.1 pad_maximum_fusion.1
  20.4 0.0 copy-start
  20.4 3.6 %fusion.15 = f32[16,17,4096]{2,1,0:T(8,128)S(1)} fusion(s32[4096]{0:T(1024)S(1)} %bitcast.33, s32[4096]{0:T(1024)S(1)} %bitcast.35, s32[4096]{0:T(1024)S(1)} %bitcast.31, s32[4096]{0:T(1024)S(1)} %bitcast.29, bf16[4096]{0:T(1024)(128)(2,1)S(1)} %get-tuple-element.6, bf16[4096]{0:T(1024)(128)(2,1)S(1)} %get-tuple-element.7, ...), kind=kOutput, calls=%fused_computation.20 | convolution fusion | flops 880803840 | bytes 4763648 | tf_op jit(solution)/shard_map/dot_general | solution.py:65
  24.0 0.0 copy-done
  24.0 1.0 %fusion.4 = f32[16,4096]{1,0:T(8,128)S(1)} fusion(bf16[16,16,4096]{2,1,0:T(8,128)(2,1)S(1)} %copy-done, f32[16,17,4096]{2,1,0:T(8,128)S(1)} %fusion.15), kind=kLoop, calls=%fused_computation.10 | loop fusion | flops 3080192 | bytes 6553600 | tf_op jit(solution)/shard_map/reduce_sum | solution.py:69
  25.0 0.5 %fusion.38 = (bf16[16,1,4096]{2,1,0:T(2,128)(2,1)S(1)}, f32[16,1,4096]{2,1,0:T(1,128)S(1)}) fusion(f32[16,17,4096]{2,1,0:T(8,128)S(1)} %fusion.15, f32[16,4096]{1,0:T(8,128)S(1)} %fusion.4), kind=kLoop, calls=%fused_computation.61 | loop fusion | flops 131072 | bytes 917504 | tf_op jit(solution)/shard_map/convert.13
  25.5 0.2 copy.31
  25.7 0.5 fusion.5
  26.2 0.0 copy-start.1
  26.2 0.0 copy-start.2
  26.2 4.1 %fusion.43 = (bf16[16,17,384]{2,1,0:T(8,128)(2,1)S(1)}, f32[16,17,384]{2,1,0:T(8,128)S(1)}) fusion(s32[4096]{0:T(1024)S(1)} %bitcast.34, s32[4096]{0:T(1024)S(1)} %bitcast.36, s32[4096]{0:T(1024)S(1)} %bitcast.32, s32[4096]{0:T(1024)S(1)} %bitcast.30, bf16[4096]{0:T(1024)(128)(2,1)S(1)} %get-tuple-element.6, bf16[4096]{0:T(1024)(128)(2,1)S(1)} %get-tuple-element.7, ...), kind=kOutput, calls=%fused_computation.66 | convolution fusion | flops 885364736 | bytes 2953216 | tf_op jit(solution)/shard_map/dot_general | solution.py:73
  30.3 0.1 fusion.40
  30.4 2.7 %collective-permute-start.4 = (bf16[16,17,64]{2,1,0:T(8,128)(2,1)S(1)}, bf16[16,17,64]{2,1,0:T(8,128)(2,1)S(1)}, u32[]{:S(2)}, u32[]{:S(2)}) collective-permute-start(bf16[16,17,64]{2,1,0:T(8,128)(2,1)S(1)} %get-tuple-element.12), channel_id=1, source_target_pairs={{0,28},{4,0},{8,4},{12,8},{16,12},{20,16},{24,20},{28,24},{1,29},{... | collective-permute-start | bytes 104456 | tf_op jit(solution)/shard_map/ppermute | solution.py:25
  33.1 0.0 collective-permute-start.5
  33.1 2.3 %collective-permute-done.4 = bf16[16,17,64]{2,1,0:T(8,128)(2,1)S(1)} collective-permute-done((bf16[16,17,64]{2,1,0:T(8,128)(2,1)S(1)}, bf16[16,17,64]{2,1,0:T(8,128)(2,1)S(1)}, u32[]{:S(2)}, u32[]{:S(2)}) %collective-permute-start.4) | collective-permute-done | bytes 34848 | tf_op jit(solution)/shard_map/ppermute | solution.py:25
  35.4 2.6 %collective-permute-done.5 = bf16[16,17,64]{2,1,0:T(8,128)(2,1)S(1)} collective-permute-done((bf16[16,17,64]{2,1,0:T(8,128)(2,1)S(1)}, bf16[16,17,64]{2,1,0:T(8,128)(2,1)S(1)}, u32[]{:S(2)}, u32[]{:S(2)}) %collective-permute-start.5) | collective-permute-done | bytes 34848 | tf_op jit(solution)/shard_map/ppermute | solution.py:25
  38.1 0.2 fusion.18
  38.3 0.0 copy-done.1
  38.4 0.1 copy.13
  38.5 0.0 copy-done.2
  38.5 0.8 %fusion.44 = (bf16[24,24,256]{2,0,1:T(8,128)(2,1)S(1)}, f32[24,24,256]{2,0,1:T(8,128)S(1)}) fusion(f32[16,24,256]{2,1,0:T(8,128)S(1)} %pad_maximum_fusion, s32[]{:T(128)S(6)} %select_n.19, s32[]{:T(128)S(6)} %select_n.20, f32[64,64]{1,0:T(8,128)S(1)} %copy-done.2), kind=kOutput, calls=%fused_computation.67 | convolution fusion | flops 28459008 | bytes 1294344 | tf_op jit(solution)/shard_map/ij,ikc->jkc/dot_general | solution.py:99
  39.3 3.5 %collective-permute-start.6 = (bf16[4,24,256]{2,0,1:T(4,128)(2,1)S(1)}, bf16[4,24,256]{2,0,1:T(4,128)(2,1)S(1)}, u32[]{:S(2)}, u32[]{:S(2)}) collective-permute-start(bf16[4,24,256]{2,0,1:T(4,128)(2,1)S(1)} %get-tuple-element.10), channel_id=1, source_target_pairs={{0,1},{1,2},{2,3},{4,5},{5,6},{6,7},{8,9},{9,10},{10,11},{12,13},{... | collective-permute-start | bytes 147464 | tf_op jit(solution)/shard_map/ppermute | solution.py:31
  42.8 1.3 %collective-permute-start.7 = (bf16[4,24,256]{2,0,1:T(4,128)(2,1)S(1)}, bf16[4,24,256]{2,0,1:T(4,128)(2,1)S(1)}, u32[]{:S(2)}, u32[]{:S(2)}) collective-permute-start(bf16[4,24,256]{2,0,1:T(4,128)(2,1)S(1)} %get-tuple-element.11), channel_id=1, source_target_pairs={{1,0},{2,1},{3,2},{5,4},{6,5},{7,6},{9,8},{10,9},{11,10},{13,12},{... | collective-permute-start | bytes 147464 | tf_op jit(solution)/shard_map/ppermute | solution.py:31
  44.1 0.4 collective-permute-done.6
  44.5 4.3 %collective-permute-done.7 = bf16[4,24,256]{2,0,1:T(4,128)(2,1)S(1)} collective-permute-done((bf16[4,24,256]{2,0,1:T(4,128)(2,1)S(1)}, bf16[4,24,256]{2,0,1:T(4,128)(2,1)S(1)}, u32[]{:S(2)}, u32[]{:S(2)}) %collective-permute-start.7) | collective-permute-done | bytes 49184 | tf_op jit(solution)/shard_map/ppermute | solution.py:31
  48.8 0.1 fusion.17
  48.9 0.9 %copy.15 = f32[16,16,256]{2,1,0:T(8,128)} copy(f32[16,16,256]{2,0,1:T(8,128)S(1)} %slice.126) | data formatting | bytes 524288
  49.8 0.7 %copy.16 = f32[16,8,256]{2,1,0:T(8,128)} copy(f32[16,8,256]{2,0,1:T(8,128)S(1)} %slice.127) | data formatting | bytes 262144
  (10 shorter events, 0.2 us)
Async XLA Ops:
  2.5 7.3 %collective-permute-start = (bf16[4,24,256]{2,0,1:T(4,128)(2,1)S(1)}, bf16[4,24,256]{2,0,1:T(4,128)(2,1)S(1)}, u32[]{:S(2)}, u32[]{:S(2)}) collective-permute-start(bf16[4,24,256]{2,0,1:T(4,128)(2,1)S(1)} %get-tuple-element.14), channel_id=1, source_target_pairs={{0,1},{1,2},{2,3},{4,5},{5,6},{6,7},{8,9},{9,10},{10,11},{12,13},{... | collective-permute-start | bytes 147464 | tf_op jit(solution)/shard_map/ppermute | solution.py:17
  7.5 6.0 %collective-permute-start.1 = (bf16[4,24,256]{2,0,1:T(4,128)(2,1)S(1)}, bf16[4,24,256]{2,0,1:T(4,128)(2,1)S(1)}, u32[]{:S(2)}, u32[]{:S(2)}) collective-permute-start(bf16[4,24,256]{2,0,1:T(4,128)(2,1)S(1)} %get-tuple-element.15), channel_id=1, source_target_pairs={{1,0},{2,1},{3,2},{5,4},{6,5},{7,6},{9,8},{10,9},{11,10},{13,12},{... | collective-permute-start | bytes 147464 | tf_op jit(solution)/shard_map/ppermute | solution.py:18
  15.5 4.7 %collective-permute-start.2 = (bf16[16,17,64]{2,0,1:T(8,128)(2,1)S(1)}, bf16[16,17,64]{2,0,1:T(8,128)(2,1)S(1)}, u32[]{:S(2)}, u32[]{:S(2)}) collective-permute-start(bf16[16,17,64]{2,0,1:T(8,128)(2,1)S(1)} %get-tuple-element.16), channel_id=1, source_target_pairs={{0,4},{4,8},{8,12},{12,16},{16,20},{20,24},{24,28},{28,0},{1,5},{5... | collective-permute-start | bytes 104456 | tf_op jit(solution)/shard_map/ppermute | solution.py:17
  15.6 4.6 %collective-permute-start.3 = (bf16[16,17,64]{2,0,1:T(8,128)(2,1)S(1)}, bf16[16,17,64]{2,0,1:T(8,128)(2,1)S(1)}, u32[]{:S(2)}, u32[]{:S(2)}) collective-permute-start(bf16[16,17,64]{2,0,1:T(8,128)(2,1)S(1)} %get-tuple-element.17), channel_id=1, source_target_pairs={{4,0},{8,4},{12,8},{16,12},{20,16},{24,20},{28,24},{0,28},{5,1},{9... | collective-permute-start | bytes 104456 | tf_op jit(solution)/shard_map/ppermute | solution.py:18
  20.4 3.6 %copy-start = (bf16[16,16,4096]{2,1,0:T(8,128)(2,1)S(1)}, bf16[16,16,4096]{2,1,0:T(8,128)(2,1)}, u32[]{:S(2)}) copy-start(bf16[16,16,4096]{2,1,0:T(8,128)(2,1)} %param.7) | copy-start | bytes 6291460
  26.2 12.2 %copy-start.1 = (bf16[16,8,256]{2,1,0:T(8,128)(2,1)S(1)}, bf16[16,8,256]{2,1,0:T(8,128)(2,1)}, u32[]{:S(2)}) copy-start(bf16[16,8,256]{2,1,0:T(8,128)(2,1)} %param.8) | copy-start | bytes 196612
  26.2 12.3 %copy-start.2 = (f32[64,64]{1,0:T(8,128)S(1)}, f32[64,64]{1,0:T(8,128)}, u32[]{:S(2)}) copy-start(f32[64,64]{1,0:T(8,128)} %param.11) | copy-start | bytes 49156
  30.4 5.0 %collective-permute-start.4 = (bf16[16,17,64]{2,1,0:T(8,128)(2,1)S(1)}, bf16[16,17,64]{2,1,0:T(8,128)(2,1)S(1)}, u32[]{:S(2)}, u32[]{:S(2)}) collective-permute-start(bf16[16,17,64]{2,1,0:T(8,128)(2,1)S(1)} %get-tuple-element.12), channel_id=1, source_target_pairs={{0,28},{4,0},{8,4},{12,8},{16,12},{20,16},{24,20},{28,24},{1,29},{... | collective-permute-start | bytes 104456 | tf_op jit(solution)/shard_map/ppermute | solution.py:25
  33.1 4.9 %collective-permute-start.5 = (bf16[16,17,64]{2,1,0:T(8,128)(2,1)S(1)}, bf16[16,17,64]{2,1,0:T(8,128)(2,1)S(1)}, u32[]{:S(2)}, u32[]{:S(2)}) collective-permute-start(bf16[16,17,64]{2,1,0:T(8,128)(2,1)S(1)} %get-tuple-element.13), channel_id=1, source_target_pairs={{0,4},{4,8},{8,12},{12,16},{16,20},{20,24},{24,28},{28,0},{1,5},{5... | collective-permute-start | bytes 104456 | tf_op jit(solution)/shard_map/ppermute | solution.py:25
  39.3 5.2 %collective-permute-start.6 = (bf16[4,24,256]{2,0,1:T(4,128)(2,1)S(1)}, bf16[4,24,256]{2,0,1:T(4,128)(2,1)S(1)}, u32[]{:S(2)}, u32[]{:S(2)}) collective-permute-start(bf16[4,24,256]{2,0,1:T(4,128)(2,1)S(1)} %get-tuple-element.10), channel_id=1, source_target_pairs={{0,1},{1,2},{2,3},{4,5},{5,6},{6,7},{8,9},{9,10},{10,11},{12,13},{... | collective-permute-start | bytes 147464 | tf_op jit(solution)/shard_map/ppermute | solution.py:31
  42.8 6.0 %collective-permute-start.7 = (bf16[4,24,256]{2,0,1:T(4,128)(2,1)S(1)}, bf16[4,24,256]{2,0,1:T(4,128)(2,1)S(1)}, u32[]{:S(2)}, u32[]{:S(2)}) collective-permute-start(bf16[4,24,256]{2,0,1:T(4,128)(2,1)S(1)} %get-tuple-element.11), channel_id=1, source_target_pairs={{1,0},{2,1},{3,2},{5,4},{6,5},{7,6},{9,8},{10,9},{11,10},{13,12},{... | collective-permute-start | bytes 147464 | tf_op jit(solution)/shard_map/ppermute | solution.py:31
where the time goes:
time: 51 us; the launch traced here: 50.5 us
  starting transfers between devices  16.4 us (32%)
  waiting for transfers between devices  14.1 us (28%)
  matrix products  9.56 us (19%)
  local copies, waits for them, and re-layouts  6.07 us (12%)
  other arithmetic  3.44 us (7%)
  between operations  0.9 us (2%)
    ppermute x2, starting transfers between devices, extended(): before = lax.ppermute(last, axis, up)  5.02 us
    ppermute x2, waiting for transfers between devices, shifted(): lax.ppermute(value, axis, [(i, (i + by) % size) for i in range(size)])  4.94 us
    ppermute x2, starting transfers between devices, from_behind(): return lax.ppermute(value, axis, pairs)  4.78 us
    ppermute x2, waiting for transfers between devices, from_behind(): return lax.ppermute(value, axis, pairs)  4.68 us
    dot_general x1, matrix products, shards(): lax.dot_general(adjoint.reshape(level_rows * kinds, fine_cells), interp_m...  4.14 us
    ppermute x2, starting transfers between devices, extended(): after = lax.ppermute(leading, axis, down)  3.92 us
    ppermute x2, waiting for transfers between devices, extended(): after = lax.ppermute(leading, axis, down)  3.61 us
    dot_general x1, matrix products, shards(): jnp.dot(flattened, interp_matrix, preferred_element_type=jnp.float32)  3.56 us
  transfers between devices with their start and end apart: 8, of which 6 were waited for; matrix products, arithmetic and copies ran while one was open for 4% of the time, Pallas kernels for 0%

commit v1 on v0

v1 whole, which is shorter than its diff:
```python
import functools

import jax
import jax.numpy as jnp
from jax import lax
from jax.experimental import pallas as pl
from jax.experimental.pallas import tpu as pltpu
from jax.sharding import PartitionSpec as P

HB = 4
CW = 64
LANE = 128
CHUNK = 1024
MESH = pl.DeviceIdType.MESH
F32 = jnp.float32
BF16 = jnp.bfloat16

DIRECTIONS = ((-1, -1), (1, -1), (-1, 1), (1, 1), (0, -1), (0, 1), (-1, 0), (1, 0))


def kernel(
    tiles, levs, pert_hbm, cp_hbm, mc_hbm, cc_hbm, vert_hbm, st_hbm, w_hbm, mo_ref, co_ref,
    mc, cc, cp, pert, vert, st, w, matrix, fld, comb, adj, inc, acc, out_buf, r_tile, r_lev, r_diag,
    mo, co, load_sem, send1, recv1, send2, recv2, store_sem,
):
    rows, members, cells = mc_hbm.shape
    group = cc_hbm.shape[1]
    total_levels = vert_hbm.shape[0]
    fine = pert_hbm.shape[2]
    span = cells + LANE
    edge = HB * members + rows
    comb_at = (rows - HB) * members
    tail_at = comb_at - HB * members

    def level_at(i):
        return (i - HB) * members if i >= HB else comb_at + rows + i * members

    t = lax.axis_index("tile")
    v = lax.axis_index("lev")
    first = v * rows
    has = {-1: v > 0, 0: None, 1: v < levs - 1}

    def when(dl, action):
        if dl == 0:
            action()
        else:
            pl.when(has[dl])(action)

    def device(dt, dl):
        return (lax.rem(t + dt + tiles, tiles), lax.rem(v + dl + levs, levs))

    own = pl.ds(HB, rows)
    loads = [
        pltpu.make_async_copy(mc_hbm, mc.at[own, :, pl.ds(0, cells)], load_sem.at[0]),
        pltpu.make_async_copy(cc_hbm, cc.at[own, :, pl.ds(0, cells)], load_sem.at[1]),
        pltpu.make_async_copy(cp_hbm, cp.at[own, :, pl.ds(0, cells)], load_sem.at[2]),
        pltpu.make_async_copy(st_hbm, st, load_sem.at[3]),
        pltpu.make_async_copy(w_hbm, w, load_sem.at[4]),
        pltpu.make_async_copy(vert_hbm, vert, load_sem.at[5]),
        pltpu.make_async_copy(pert_hbm, pert, load_sem.at[6]),
    ]
    for load in loads:
        load.start()

    barrier = pltpu.get_barrier_semaphore()
    for dt, dl in DIRECTIONS:
        when(
            dl,
            lambda dt=dt, dl=dl: pl.semaphore_signal(
                barrier, inc=1, device_id=device(dt, dl), device_id_type=MESH
            ),
        )

    level_src = {0: (HB, rows), 1: (rows, HB), -1: (HB, HB)}
    level_dst = {0: HB, 1: 0, -1: HB + rows}
    lane_src = {0: (0, cells), 1: (cells - LANE, LANE), -1: (0, LANE)}
    lane_dst = {0: 0, 1: cells + LANE, -1: cells}
    round1 = []
    for dt, dl in DIRECTIONS:
        for buf in (mc, cc, cp):
            if buf is cp and dt != 0 and dl != 0:
                continue
            n = len(round1)
            (l0, ln), (c0, cn) = level_src[dl], lane_src[dt]
            copy = pltpu.make_async_remote_copy(
                src_ref=buf.at[pl.ds(l0, ln), :, pl.ds(c0, cn)],
                dst_ref=buf.at[pl.ds(level_dst[dl], ln), :, pl.ds(lane_dst[dt], cn)],
                send_sem=send1.at[n],
                recv_sem=recv1.at[n],
                device_id=device(dt, dl),
                device_id_type=MESH,
            )
            round1.append((dl, copy))

    @pl.when(v == 0)
    def _():
        for buf in (mc, cc, cp):
            buf[0:HB] = jnp.zeros((HB,) + buf.shape[1:], BF16)
        r_lev[0] = jnp.zeros(r_lev.shape[1:], BF16)
        r_diag[0] = jnp.zeros(r_diag.shape[1:], BF16)

    @pl.when(v == levs - 1)
    def _():
        for buf in (mc, cc, cp):
            buf[HB + rows :] = jnp.zeros((HB,) + buf.shape[1:], BF16)
        r_lev[1] = jnp.zeros(r_lev.shape[1:], BF16)
        r_diag[1] = jnp.zeros(r_diag.shape[1:], BF16)

    for load in loads[:3]:
        load.wait()
    neighbours = 2 + 3 * jnp.where(v > 0, 1, 0) + 3 * jnp.where(v < levs - 1, 1, 0)
    pl.semaphore_wait(barrier, neighbours)
    for dl, copy in round1:
        when(dl, copy.start)

    for load in loads[3:6]:
        load.wait()
    pack = 16
    base_rows = lax.broadcasted_iota(jnp.int32, (pack, LANE), 0).astype(jnp.int16)

    def build(step, carry):
        lanes = pl.ds(pl.multiple_of(step * LANE, LANE), LANE)
        places, weights = [], []
        for corner in range(4):
            cell = st[corner : corner + 1, lanes] - CW
            cell = jnp.where(cell < 0, cell + span, cell)
            places.append(jnp.broadcast_to(cell, (pack, LANE)).astype(jnp.int16))
            weight = w[corner : corner + 1, lanes].astype(F32)
            weights.append(jnp.broadcast_to(weight, (pack, LANE)).astype(BF16))
        for block in range(span // pack):
            index = base_rows + jnp.int16(block * pack)
            value = jnp.zeros((pack, LANE), BF16)
            for corner in range(4):
                value = jnp.where(places[corner] == index, weights[corner], value)
            matrix[block * pack : (block + 1) * pack, lanes] = value
        return carry

    lax.fori_loop(0, fine // LANE, build, 0)

    for dl, copy in round1:
        when(-dl, copy.wait_recv)

    next_side = lax.broadcasted_iota(jnp.int32, (1, LANE), 1) < LANE - CW

    def window(buf, level, lane_tile):
        if lane_tile * LANE < cells:
            return buf[level, :, lane_tile * LANE : (lane_tile + 1) * LANE].astype(F32)
        from_next = buf[level, :, cells : cells + LANE].astype(F32)
        from_prev = buf[level, :, cells + LANE : cells + 2 * LANE].astype(F32)
        return jnp.where(next_side, from_next, from_prev)

    def factor(i, j):
        return vert[
            lax.rem(first + i + total_levels, total_levels),
            lax.rem(first + j + total_levels, total_levels),
        ]

    for lane_tile in range(span // LANE):
        lanes = slice(lane_tile * LANE, (lane_tile + 1) * LANE)
        values = [window(mc, level, lane_tile) for level in range(rows + 2 * HB)]
        for i in range(rows):
            total = factor(i, i - HB) * values[i]
            for d in range(1, 2 * HB + 1):
                total = total + factor(i, i + d - HB) * values[i + d]
            at = level_at(i)
            fld[at : at + members, lanes] = total.astype(BF16)
        values = [window(cc, level, lane_tile) for level in range(rows + 2 * HB)]
        for i in range(rows):
            total = factor(i, i - HB) * values[i]
            for d in range(1, 2 * HB + 1):
                total = total + factor(i, i + d - HB) * values[i + d]
            total = total.astype(BF16).astype(F32) * window(cp, i + HB, lane_tile)
            comb[i : i + 1, lanes] = jnp.sum(total, axis=0, keepdims=True)
    fld[comb_at : comb_at + rows, :] = comb[...].astype(BF16)

    loads[6].wait()
    for chunk in range(fine // CHUNK):
        lanes = slice(chunk * CHUNK, (chunk + 1) * CHUNK)
        interp = jnp.dot(fld[...], matrix[:, lanes], preferred_element_type=F32)
        for i in range(rows):
            at = level_at(i)
            member = pert[i, :, lanes].astype(F32)
            line = jnp.sum(member * interp[at : at + members], axis=0, keepdims=True)
            line = line + interp[comb_at + i : comb_at + i + 1]
            adj[at : at + members, lanes] = (member * line).astype(BF16)
            inc[i : i + 1, lanes] = line
        adj[comb_at : comb_at + rows, lanes] = inc[:, lanes].astype(BF16)
        back = lax.dot_general(
            adj[:, lanes], matrix[:, lanes], (((1,), (1,)), ((), ())), preferred_element_type=F32
        )
        if chunk == 0:
            acc[...] = back
        else:
            acc[...] += back
    out_buf[...] = acc[...].astype(BF16)

    row_src = {0: (0, acc.shape[0]), 1: (tail_at, edge), -1: (comb_at, edge)}
    round2 = []
    for n, (dt, dl) in enumerate(DIRECTIONS):
        r0, rn = row_src[dl]
        side, floor = (1 - dt) // 2, (1 - dl) // 2
        if dt == 0:
            src, dst = out_buf.at[pl.ds(r0, rn), pl.ds(0, cells)], r_lev.at[floor]
        else:
            src = out_buf.at[pl.ds(r0, rn), pl.ds(cells, LANE)]
            dst = r_tile.at[side] if dl == 0 else r_diag.at[floor, side]
        copy = pltpu.make_async_remote_copy(
            src_ref=src,
            dst_ref=dst,
            send_sem=send2.at[n],
            recv_sem=recv2.at[n],
            device_id=device(dt, dl),
            device_id_type=MESH,
        )
        round2.append((dl, copy))
    for dl, copy in round2:
        when(dl, copy.start)
    for dl, copy in round2:
        when(-dl, copy.wait_recv)

    tile_lanes = lax.broadcasted_iota(jnp.int32, (1, LANE), 1)
    for lane_tile in range(cells // LANE):
        lanes = slice(lane_tile * LANE, (lane_tile + 1) * LANE)

        def joined(base, prev, following):
            if lane_tile == 0:
                base = base + jnp.where(tile_lanes < CW, prev.astype(F32), 0.0)
            if lane_tile == cells // LANE - 1:
                base = base + jnp.where(tile_lanes >= LANE - CW, following.astype(F32), 0.0)
            return base

        def halo(floor, r0, rn):
            at = slice(r0, r0 + rn)
            return joined(
                r_lev[floor, at, lanes].astype(F32), r_diag[floor, 0, at, :], r_diag[floor, 1, at, :]
            )

        def inner(r0, rn):
            at = slice(r0, r0 + rn)
            return joined(acc[at, lanes], r_tile[0, at, :], r_tile[1, at, :])

        values = [halo(0, i * members, members) for i in range(HB)]
        values += [inner(level_at(i), members) for i in range(rows)]
        values += [halo(1, rows + i * members, members) for i in range(HB)]
        for j in range(rows):
            total = factor(j - HB, j) * values[j]
            for d in range(1, 2 * HB + 1):
                total = total + factor(j + d - HB, j) * values[j + d]
            mo[j, :, lanes] = total
        below = halo(0, HB * members, rows)
        middle = inner(comb_at, rows)
        above = halo(1, 0, rows)
        lines = [below[rows - HB + i : rows - HB + i + 1] for i in range(HB)]
        lines += [middle[i : i + 1] for i in range(rows)]
        lines += [above[i : i + 1] for i in range(HB)]
        values = [
            cp[level, :, lanes].astype(F32) * lines[level] for level in range(rows + 2 * HB)
        ]
        for j in range(rows):
            total = factor(j - HB, j) * values[j]
            for d in range(1, 2 * HB + 1):
                total = total + factor(j + d - HB, j) * values[j + d]
            co[j, :, lanes] = total

    stores = [
        pltpu.make_async_copy(mo, mo_ref, store_sem.at[0]),
        pltpu.make_async_copy(co, co_ref, store_sem.at[1]),
    ]
    for store in stores:
        store.start()
    for dl, copy in round1 + round2:
        when(dl, copy.wait_send)
    for store in stores:
        store.wait()


def solution(mesh):
    tiles, levs = mesh.shape["tile"], mesh.shape["lev"]

    def step(members_pert, coarse_pert, member_ctrl, coarse_ctrl, vert_loc, stencil, interp_w):
        rows, members, cells = member_ctrl.shape
        group = coarse_ctrl.shape[1]
        fine = members_pert.shape[2]
        levels, span, lines = rows + 2 * HB, cells + LANE, rows * (members + 1)
        edge = HB * members + rows
        hbm = pl.BlockSpec(memory_space=pl.ANY)
        copies = 8 * 2 + 4
        return pl.pallas_call(
            functools.partial(kernel, tiles, levs),
            out_shape=(
                jax.ShapeDtypeStruct((rows, members, cells), F32),
                jax.ShapeDtypeStruct((rows, group, cells), F32),
            ),
            in_specs=[hbm] * 7,
            out_specs=(hbm, hbm),
            scratch_shapes=[
                pltpu.VMEM((levels, members, cells + 2 * LANE), BF16),
                pltpu.VMEM((levels, group, cells + 2 * LANE), BF16),
                pltpu.VMEM((levels, group, cells + 2 * LANE), BF16),
                pltpu.VMEM((rows, members, fine), BF16),
                pltpu.SMEM(vert_loc.shape, F32),
                pltpu.VMEM(stencil.shape, jnp.int32),
                pltpu.VMEM(interp_w.shape, BF16),
                pltpu.VMEM((span, fine), BF16),
                pltpu.VMEM((lines, span), BF16),
                pltpu.VMEM((rows, span), F32),
                pltpu.VMEM((lines, fine), BF16),
                pltpu.VMEM((rows, fine), F32),
                pltpu.VMEM((lines, span), F32),
                pltpu.VMEM((lines, span), BF16),
                pltpu.VMEM((2, lines, LANE), BF16),
                pltpu.VMEM((2, edge, cells), BF16),
                pltpu.VMEM((2, 2, edge, LANE), BF16),
                pltpu.VMEM((rows, members, cells), F32),
                pltpu.VMEM((rows, group, cells), F32),
                pltpu.SemaphoreType.DMA((7,)),
                pltpu.SemaphoreType.DMA((copies,)),
                pltpu.SemaphoreType.DMA((copies,)),
                pltpu.SemaphoreType.DMA((8,)),
                pltpu.SemaphoreType.DMA((8,)),
                pltpu.SemaphoreType.DMA((2,)),
            ],
            compiler_params=pltpu.CompilerParams(
                collective_id=0, has_side_effects=True, vmem_limit_bytes=60 * 1024 * 1024
            ),
        )(members_pert, coarse_pert, member_ctrl, coarse_ctrl, vert_loc, stencil, interp_w)

    in_specs = (
        P("lev", None, "tile"),
        P("lev", None, "tile"),
        P("lev", None, "tile"),
        P("lev", None, "tile"),
        P(),
        P(None, "tile"),
        P(None, "tile"),
    )
    out_specs = (P("lev", None, "tile"), P("lev", None, "tile"))
    return jax.shard_map(step, mesh=mesh, in_specs=in_specs, out_specs=out_specs, check_vma=False)
```

time: 51 us -> 23.9 us (0.47)
  Pallas kernels: 0 us -> 19.9 us
  starting transfers between devices: 16.4 us -> 0 us
  waiting for transfers between devices: 14.1 us -> 0 us
  matrix products: 9.56 us -> 0 us
  other arithmetic: 3.44 us -> 0 us
  local copies, waits for them, and re-layouts: 6.07 us -> 3.24 us
    pallas_call x0 -> x1, Pallas kernels: none -> 19.9 us  [step(): pl.pallas_call(functools.partial(kernel, tiles, levs), out_shape=(jax.Sha...]
    ppermute x8 -> x0, starting transfers between devices: 16.4 us -> none  [the longest x2 5.02 us: extended(): before = lax.ppermute(last, axis, up)]
    ppermute x8 -> x0, waiting for transfers between devices: 14.1 us -> none  [the longest x2 4.94 us: shifted(): lax.ppermute(value, axis, [(i, (i + by) % size) for i in range(size)])]
    dot_general x4 -> x0, matrix products: 9.56 us -> none  [the longest x1 4.14 us: shards(): lax.dot_general(adjoint.reshape(level_rows * kinds, fine_cells), interp_m...]
    slice x10 -> x0, local copies, waits for them, and re-layouts: 2.41 us -> none  [the longest x1 1.1 us: shards(): interp_w[corner][None, :]]
    reduce_sum x2 -> x0, other arithmetic: 1.86 us -> none  [the longest x1 0.99 us: shards(): jnp.sum(pert_float * interp[:, :members], axis=1) + interp[:, members]]
    another operation x2 -> x0, other arithmetic: 1.02 us -> none
    concatenate x1 -> x0, local copies, waits for them, and re-layouts: 0.86 us -> none  [shards(): stacked = jnp.concatenate([member_ctrl, coarse_ctrl], axis=1)]
  transfers between devices with their start and end apart: 8 -> 0, of which waited for: 6 -> 0; matrix products, arithmetic and copies ran while one was open for 4% -> 0% of each run, Pallas kernels for 0% -> 0%
where the time goes in v1:
time: 23.9 us; the launch traced here: 23.8 us
  Pallas kernels  19.9 us (83%)
  local copies, waits for them, and re-layouts  3.24 us (14%)
  between operations  0.64 us (3%)
    pallas_call x1, Pallas kernels, step(): pl.pallas_call(functools.partial(kernel, tiles, levs), out_shape=(jax.Sha...  19.9 us
    unnamed x2, local copies, waits for them, and re-layouts  3.24 us

profile of v1, /device:TPU:0, one launch (start us, length us, event | category | flops | bytes accessed | tf_op | source)
XLA Modules:
  0.0 23.8 jit_solution(14310530079809321791)
XLA Ops:
  0.6 19.9 %shard_map.86 = (f32[16,16,256]{2,1,0:T(8,128)}, f32[16,8,256]{2,1,0:T(8,128)}) custom-call(bf16[16,16,4096]{2,1,0:T(8,128)(2,1)} %pert_hbm.1, bf16[16,8,256]{2,1,0:T(8,128)(2,1)} %cp_hbm.1, bf16[16,16,256]{2,1,0:T(8,128)(2,1)} %mc_hbm.1, bf16[16,8,256]{2,1,0:T(8,128)(2,1)} %cc_hbm.1, f32[64,64]{1,0:T(8,128)} %vert_hbm.1, s32[4,4096]{1,0:T(4,128)} %st_hbm.1, ...), custom_call_target="tpu_custom_call" | custom-call | tf_op jit(solution)/shard_map/pallas_call | solution.py:288
  20.5 1.7 %copy.11 = f32[16,16,256]{2,1,0:T(8,128)} copy(f32[16,16,256]{2,1,0:T(8,128)} %get-tuple-element.4) | data formatting | bytes 524288
  22.2 1.6 %copy.12 = f32[16,8,256]{2,1,0:T(8,128)} copy(f32[16,8,256]{2,1,0:T(8,128)} %get-tuple-element.5) | data formatting | bytes 262144

commit v2 on v1

--- a/solution.py
+++ b/solution.py
@@ -15,13 +15,13 @@
 F32 = jnp.float32
 BF16 = jnp.bfloat16
 
-DIRECTIONS = ((-1, -1), (1, -1), (-1, 1), (1, 1), (0, -1), (0, 1), (-1, 0), (1, 0))
+DIRECTIONS = ((0, -1), (0, 1), (-1, 0), (1, 0), (-1, -1), (1, -1), (-1, 1), (1, 1))
 
 
 def kernel(
-    tiles, levs, pert_hbm, cp_hbm, mc_hbm, cc_hbm, vert_hbm, st_hbm, w_hbm, mo_ref, co_ref,
+    tiles, levs, pert_hbm, cp_hbm, mc_hbm, cc_hbm, vert_hbm, st_hbm, w_hbm, mo, co,
     mc, cc, cp, pert, vert, st, w, matrix, fld, comb, adj, inc, acc, out_buf, r_tile, r_lev, r_diag,
-    mo, co, load_sem, send1, recv1, send2, recv2, store_sem,
+    load_sem, send1, recv1, send2, recv2,
 ):
     rows, members, cells = mc_hbm.shape
     group = cc_hbm.shape[1]
@@ -75,22 +75,25 @@
     level_dst = {0: HB, 1: 0, -1: HB + rows}
     lane_src = {0: (0, cells), 1: (cells - LANE, LANE), -1: (0, LANE)}
     lane_dst = {0: 0, 1: cells + LANE, -1: cells}
+    wanted = [(buf, direction) for direction in DIRECTIONS for buf in (mc, cc)]
+    wanted += [(cp, direction) for direction in ((-1, 0), (1, 0), (0, -1), (0, 1))]
     round1 = []
-    for dt, dl in DIRECTIONS:
-        for buf in (mc, cc, cp):
-            if buf is cp and dt != 0 and dl != 0:
-                continue
-            n = len(round1)
-            (l0, ln), (c0, cn) = level_src[dl], lane_src[dt]
-            copy = pltpu.make_async_remote_copy(
-                src_ref=buf.at[pl.ds(l0, ln), :, pl.ds(c0, cn)],
-                dst_ref=buf.at[pl.ds(level_dst[dl], ln), :, pl.ds(lane_dst[dt], cn)],
-                send_sem=send1.at[n],
-                recv_sem=recv1.at[n],
-                device_id=device(dt, dl),
-                device_id_type=MESH,
-            )
-            round1.append((dl, copy))
+    for n, (buf, (dt, dl)) in enumerate(wanted):
+        (l0, ln), (c0, cn) = level_src[dl], lane_src[dt]
+        copy = pltpu.make_async_remote_copy(
+            src_ref=buf.at[pl.ds(l0, ln), :, pl.ds(c0, cn)],
+            dst_ref=buf.at[pl.ds(level_dst[dl], ln), :, pl.ds(lane_dst[dt], cn)],
+            send_sem=send1.at[n],
+            recv_sem=recv1.at[n],
+            device_id=device(dt, dl),
+            device_id_type=MESH,
+        )
+        round1.append((dl, copy))
+    needed = {"own": round1[:4], "rim": round1[4:-2], "spread": round1[-2:]}
+
+    def arrive(stage):
+        for dl, copy in needed[stage]:
+            when(-dl, copy.wait_recv)
 
     @pl.when(v == 0)
     def _():
@@ -137,9 +140,6 @@
 
     lax.fori_loop(0, fine // LANE, build, 0)
 
-    for dl, copy in round1:
-        when(-dl, copy.wait_recv)
-
     next_side = lax.broadcasted_iota(jnp.int32, (1, LANE), 1) < LANE - CW
 
     def window(buf, level, lane_tile):
@@ -156,6 +156,10 @@
         ]
 
     for lane_tile in range(span // LANE):
+        if lane_tile == 0:
+            arrive("own")
+        if lane_tile * LANE == cells:
+            arrive("rim")
         lanes = slice(lane_tile * LANE, (lane_tile + 1) * LANE)
         values = [window(mc, level, lane_tile) for level in range(rows + 2 * HB)]
         for i in range(rows):
@@ -215,6 +219,7 @@
         round2.append((dl, copy))
     for dl, copy in round2:
         when(dl, copy.start)
+    arrive("spread")
     for dl, copy in round2:
         when(-dl, copy.wait_recv)
 
@@ -262,16 +267,19 @@
                 total = total + factor(j + d - HB, j) * values[j + d]
             co[j, :, lanes] = total
 
-    stores = [
-        pltpu.make_async_copy(mo, mo_ref, store_sem.at[0]),
-        pltpu.make_async_copy(co, co_ref, store_sem.at[1]),
-    ]
-    for store in stores:
-        store.start()
     for dl, copy in round1 + round2:
         when(dl, copy.wait_send)
-    for store in stores:
-        store.wait()
+
+
+def store(mo, co, mo_hbm, co_hbm, sem):
+    copies = [
+        pltpu.make_async_copy(mo, mo_hbm, sem.at[0]),
+        pltpu.make_async_copy(co, co_hbm, sem.at[1]),
+    ]
+    for copy in copies:
+        copy.start()
+    for copy in copies:
+        copy.wait()
 
 
 def solution(mesh):
@@ -285,14 +293,15 @@
         edge = HB * members + rows
         hbm = pl.BlockSpec(memory_space=pl.ANY)
         copies = 8 * 2 + 4
-        return pl.pallas_call(
+        vmem = pl.BlockSpec(memory_space=pltpu.VMEM)
+        results = pl.pallas_call(
             functools.partial(kernel, tiles, levs),
             out_shape=(
-                jax.ShapeDtypeStruct((rows, members, cells), F32),
-                jax.ShapeDtypeStruct((rows, group, cells), F32),
+                pltpu.VMEM((rows, members, cells), F32),
+                pltpu.VMEM((rows, group, cells), F32),
             ),
             in_specs=[hbm] * 7,
-            out_specs=(hbm, hbm),
+            out_specs=(vmem, vmem),
             scratch_shapes=[
                 pltpu.VMEM((levels, members, cells + 2 * LANE), BF16),
                 pltpu.VMEM((levels, group, cells + 2 * LANE), BF16),
@@ -311,19 +320,27 @@
                 pltpu.VMEM((2, lines, LANE), BF16),
                 pltpu.VMEM((2, edge, cells), BF16),
                 pltpu.VMEM((2, 2, edge, LANE), BF16),
-                pltpu.VMEM((rows, members, cells), F32),
-                pltpu.VMEM((rows, group, cells), F32),
                 pltpu.SemaphoreType.DMA((7,)),
                 pltpu.SemaphoreType.DMA((copies,)),
                 pltpu.SemaphoreType.DMA((copies,)),
                 pltpu.SemaphoreType.DMA((8,)),
                 pltpu.SemaphoreType.DMA((8,)),
-                pltpu.SemaphoreType.DMA((2,)),
             ],
             compiler_params=pltpu.CompilerParams(
                 collective_id=0, has_side_effects=True, vmem_limit_bytes=60 * 1024 * 1024
             ),
         )(members_pert, coarse_pert, member_ctrl, coarse_ctrl, vert_loc, stencil, interp_w)
+        return pl.pallas_call(
+            store,
+            out_shape=(
+                jax.ShapeDtypeStruct((rows, members, cells), F32),
+                jax.ShapeDtypeStruct((rows, group, cells), F32),
+            ),
+            in_specs=[vmem, vmem],
+            out_specs=(hbm, hbm),
+            scratch_shapes=[pltpu.SemaphoreType.DMA((2,))],
+            compiler_params=pltpu.CompilerParams(vmem_limit_bytes=1024 * 1024),
+        )(*results)
 
     in_specs = (
         P("lev", None, "tile"),

time: 23.9 us -> 20.5 us (0.86)
  local copies, waits for them, and re-layouts: 3.24 us -> 0 us
    unnamed x2 -> x0, local copies, waits for them, and re-layouts: 3.24 us -> none
    pallas_call x1 -> x2, Pallas kernels: 19.9 us -> 19.7 us  [the longest x1 18.9 us: step(): pl.pallas_call(functools.partial(kernel, tiles, levs), out_shape=(pltpu.V...]
where the time goes in v2:
time: 20.5 us; the launch traced here: 20.3 us
  Pallas kernels  19.7 us (96%)
  between operations  0.64 us (3%)
    pallas_call x1, Pallas kernels, step(): pl.pallas_call(functools.partial(kernel, tiles, levs), out_shape=(pltpu.V...  18.9 us
    pallas_call x1, Pallas kernels, step(): pl.pallas_call(store, out_shape=(jax.ShapeDtypeStruct((rows, members, cel...  0.76 us

profile of v2, /device:TPU:0, one launch (start us, length us, event | category | flops | bytes accessed | tf_op | source)
XLA Modules:
  0.0 20.3 jit_solution(8155824045106535355)
XLA Ops:
  0.6 18.9 %shard_map.86 = (f32[16,16,256]{2,1,0:T(8,128)S(1)}, f32[16,8,256]{2,1,0:T(8,128)S(1)}) custom-call(bf16[16,16,4096]{2,1,0:T(8,128)(2,1)} %pert_hbm.1, bf16[16,8,256]{2,1,0:T(8,128)(2,1)} %cp_hbm.1, bf16[16,16,256]{2,1,0:T(8,128)(2,1)} %mc_hbm.1, bf16[16,8,256]{2,1,0:T(8,128)(2,1)} %cc_hbm.1, f32[64,64]{1,0:T(8,128)} %vert_hbm.1, s32[4,4096]{1,0:T(4,128)} %st_hbm.1, ...), custom_call_target="tpu_custom_call" | custom-call | tf_op jit(solution)/shard_map/pallas_call | solution.py:297
  19.6 0.8 %shard_map.87 = (f32[16,16,256]{2,1,0:T(8,128)}, f32[16,8,256]{2,1,0:T(8,128)}) custom-call(f32[16,16,256]{2,1,0:T(8,128)S(1)} %get-tuple-element.4.mo, f32[16,8,256]{2,1,0:T(8,128)S(1)} %get-tuple-element.5.co), custom_call_target="tpu_custom_call" | custom-call | tf_op jit(solution)/shard_map/pallas_call | solution.py:333
